TPU v7x, 1024 devices: a whole 8x8x8 slice. The times are simulated.
1024 devices in a mesh: section: 128 (over y, x, z_lo), tp: 8 (over z_hi, core).
Axes of the slice: x: 8, y: 8, z: 8 (z_hi: 4, z_lo: 2; z = z_hi * 2 + z_lo), core: 2. Of those that a mesh axis runs over, the one named last changes fastest.
Arguments:
- stash: bfloat16 [128, 2, 512, 4096], P('section', None, 'tp'), may hold values from -660 to 660
- slot: int32 [128], P('section'), may hold values from 0 to 1
- doc_ids: int32 [128, 2, 512], P('section', None, 'tp'), may hold values from 0 to 3, never falling along the last dimension, each value on 1 to 256 neighbouring positions
- norm_gain: bfloat16 [4096], replicated, may hold values from 0.099609375 to 1.8984375
- w_query: bfloat16 [4096, 4096], P(None, 'tp'), may hold values from -21 to 21
- w_key: bfloat16 [4096, 1024], P(None, 'tp'), may hold values from -21 to 21
- value_weight: bfloat16 [4096, 1024], P(None, 'tp'), may hold values from -0.09375 to 0.09375
Outputs:
- received: bfloat16 [128, 512, 4096], P('section', None, 'tp')
Inputs may be any that keep to these rules, and one draw needn't show every extreme that they name: `doc_ids`: document numbers never fall along a micro-batch.
All inputs are finite; a program needn't handle non-finite values.
Results may differ from a plain program's by a relative error of at most 0.025.
The roundings to bfloat16 on the way count: a program that leaves them out, or rounds other values in their place, can miss the bound.
Values may be sent and summed in bfloat16 or wider, within the bound.
No kernel may reach another device: no remote copies, remote signals or barrier semaphores. Data moves between devices by JAX's collectives and lax.ppermute only.
A program may use at most 64 MiB of HBM per device.

v0:
```python
import functools
import math

import jax
import jax.numpy as jnp
import numpy as np
from jax import lax
from jax.experimental import pallas as pl
from jax.experimental.pallas import tpu as pltpu
from jax.sharding import PartitionSpec as P

HEAD_SIZE = 128
LANES = 128
ROPE_BASE = 500000.0
NORM_EPSILON = 1e-05
AXES = ("section", "tp")
VMEM = pltpu.MemorySpace.VMEM


def fetch(source, target, sem):
    return pltpu.make_async_copy(source, target, sem)


def normalize_kernel(
    slot_ref, stash_ref, doc_ref, gain_ref, out_ref, docs, gain_buf, buf, sems
):
    rows, width = buf.shape
    pieces = sems.shape[0] - 2
    step = rows // pieces
    pick = slot_ref[0]
    copies = [
        fetch(doc_ref, docs, sems.at[0]),
        fetch(gain_ref, gain_buf, sems.at[1]),
    ]
    for i in range(pieces):
        part = pl.ds(i * step, step)
        copies.append(fetch(stash_ref.at[0, pick, part], buf.at[part], sems.at[2 + i]))
    for copy in copies:
        copy.start()
    for copy in copies[:2]:
        copy.wait()
    numbers = docs[0, pl.ds(pick, 1), :].astype(jnp.float32)
    row = lax.broadcasted_iota(jnp.int32, (rows, rows), 0)
    column = lax.broadcasted_iota(jnp.int32, (rows, rows), 1)
    upright = jnp.sum(jnp.where(row == column, numbers, 0.0), axis=1, keepdims=True)
    out_ref[:, width:] = jnp.broadcast_to(upright, (rows, LANES)).astype(jnp.bfloat16)
    gain = gain_buf[...].astype(jnp.float32)
    for i in range(pieces):
        copies[2 + i].wait()
        part = slice(i * step, (i + 1) * step)
        x = buf[part, :].astype(jnp.float32)
        scale = lax.rsqrt(jnp.mean(x * x, axis=-1, keepdims=True) + NORM_EPSILON)
        for j in range(width // LANES):
            lanes = slice(j * LANES, (j + 1) * LANES)
            scaled = x[:, lanes] * scale * gain[j : j + 1, :]
            out_ref[part, lanes] = scaled.astype(jnp.bfloat16)


def normalize(slot, stash, doc_ids, gain):
    rows, width = stash.shape[2:]
    pieces = 4
    hbm = pl.BlockSpec(memory_space=pltpu.MemorySpace.HBM)

    def stay(x):
        return pltpu.with_memory_space_constraint(x, pltpu.MemorySpace.HBM)

    return pl.pallas_call(
        normalize_kernel,
        out_shape=jax.ShapeDtypeStruct((rows, width + LANES), jnp.bfloat16),
        in_specs=[pl.BlockSpec(memory_space=pltpu.MemorySpace.SMEM)] + [hbm] * 3,
        out_specs=pl.BlockSpec(memory_space=VMEM),
        scratch_shapes=[
            pltpu.VMEM(doc_ids.shape, doc_ids.dtype),
            pltpu.VMEM((width // LANES, LANES), gain.dtype),
            pltpu.VMEM((rows, width), jnp.bfloat16),
            pltpu.SemaphoreType.DMA((2 + pieces,)),
        ],
        compiler_params=pltpu.CompilerParams(vmem_limit_bytes=8 << 20),
    )(slot, stay(stash), stay(doc_ids), stay(gain.reshape(-1, LANES)))


def tables_kernel(inverse_ref, cosine, sine):
    rows = cosine.shape[0]
    position = lax.broadcasted_iota(jnp.int32, (rows, LANES), 0).astype(jnp.float32)
    lane = lax.broadcasted_iota(jnp.int32, (rows, LANES), 1)
    angle = position * inverse_ref[...]
    cosine[...] = jnp.cos(angle)
    turned = jnp.sin(angle)
    sine[...] = jnp.where(lane < HEAD_SIZE // 2, -turned, turned)


def tables(total):
    exponent = -2.0 * np.arange(HEAD_SIZE // 2) / HEAD_SIZE
    inverse = np.tile(ROPE_BASE**exponent, 2)[None].astype(np.float32)
    vmem = pl.BlockSpec(memory_space=VMEM)
    shape = jax.ShapeDtypeStruct((total, LANES), jnp.float32)
    return pl.pallas_call(
        tables_kernel,
        out_shape=(shape, shape),
        in_specs=[vmem],
        out_specs=(vmem, vmem),
        compiler_params=pltpu.CompilerParams(vmem_limit_bytes=8 << 20),
        cost_estimate=pl.CostEstimate(flops=4 << 20, bytes_accessed=1 << 20, transcendentals=0),
    )(inverse)


def granule(chip_shift, mine, swapped):
    t, odd = lax.axis_index("tp"), 1 - lax.axis_index("section") % 2
    core, chips = t % 2, lax.axis_size("tp") // 2
    up = core if mine else 1 - core
    chip = lax.rem(t // 2 - odd + chips + jnp.where(up == 0, -chip_shift, 1 + chip_shift), chips)
    return 2 * chip + (1 - up if swapped else up)


def project_to(pieces, weights, cosine, sine, store):
    w_query, w_key, w_value = weights
    width = w_query.shape[0]
    rows = pieces[0][0].shape[0]
    x = jnp.concatenate([block[:, :width] for block, _ in pieces], axis=0)
    w_both = jnp.concatenate([w_key[...], w_value[...]], axis=1)
    products = [
        jnp.dot(x, w, preferred_element_type=jnp.float32)
        for w in (w_query[:, :256], w_query[:, 256:], w_both)
    ]
    for index, (block, number) in enumerate(pieces):
        at = pl.ds(pl.multiple_of(number * rows, rows), rows)
        cos, sin = cosine[at, :], sine[at, :]
        for head in range(6):
            values = products[head // 2][index * rows : (index + 1) * rows]
            values = values[:, (head % 2) * 128 : (head % 2) * 128 + 128]
            if head < 5:
                values = values * cos + pltpu.roll(values, 64, 1) * sin
            store(index, at, head * 128, values.astype(jnp.bfloat16))
        store(index, at, 768, block[:, width:])


def project_kernel(where, b0, b1, w_query, w_key, w_value, cosine, sine, out_ref):
    rows = b0.shape[0]

    def store(index, at, column, values):
        out_ref[index * rows : (index + 1) * rows, column : column + 128] = values

    pieces = [(block, granule(*place)) for block, place in zip((b0, b1), where)]
    project_to(pieces, (w_query, w_key, w_value), cosine, sine, store)


def project(where, blocks, weights, cosine, sine):
    rows = blocks[0].shape[0]
    vmem = pl.BlockSpec(memory_space=VMEM)
    flops = 2 * 2 * rows * weights[0].shape[0] * 768
    return pl.pallas_call(
        functools.partial(project_kernel, where),
        out_shape=jax.ShapeDtypeStruct((2 * rows, 768 + LANES), jnp.bfloat16),
        in_specs=[vmem] * 7,
        out_specs=vmem,
        compiler_params=pltpu.CompilerParams(vmem_limit_bytes=16 << 20),
        cost_estimate=pl.CostEstimate(flops=flops, bytes_accessed=8 << 20, transcendentals=0),
    )(*blocks, *weights, cosine, sine)


def attend_kernel(
    where, e0, e1, e2, b0, b1, w_query, w_key, w_value, cosine, sine, out_ref, rows_ref
):
    rows = b0.shape[0]

    def store(index, at, column, values):
        rows_ref[at, column : column + 128] = values

    for pair, early in zip(where, (e0, e1, e2)):
        for index, place in enumerate(pair):
            at = pl.ds(pl.multiple_of(granule(*place) * rows, rows), rows)
            rows_ref[at, :] = early[index * rows : (index + 1) * rows, :]
    pieces = [(block, granule(*place)) for block, place in zip((b0, b1), where[3])]
    project_to(pieces, (w_query, w_key, w_value), cosine, sine, store)

    total = rows_ref.shape[0]
    heads, tile = 4, 128
    factor = math.log2(math.e) / math.sqrt(HEAD_SIZE)
    contract_last = (((1,), (1,)), ((), ()))
    ones = jnp.ones((8, LANES), jnp.bfloat16)
    lying = lax.dot_general(
        ones, rows_ref[:, 768:], contract_last, preferred_element_type=jnp.float32
    )[:1, :]
    scores = []
    for i in range(total // tile):
        here = slice(i * tile, (i + 1) * tile)
        queries = [rows_ref[here, h * 128 : (h + 1) * 128] for h in range(heads)]
        scores.append(
            lax.dot_general(
                jnp.concatenate(queries, axis=0),
                rows_ref[: (i + 1) * tile, 512:640],
                contract_last,
                preferred_element_type=jnp.float32,
            )
        )
    for i in range(total // tile):
        seen = (i + 1) * tile
        here = slice(i * tile, seen)
        upright = rows_ref[here, 768:769].astype(jnp.float32) * float(LANES)
        row = lax.broadcasted_iota(jnp.int32, (tile, seen), 0) + i * tile
        column = lax.broadcasted_iota(jnp.int32, (tile, seen), 1)
        allowed = (column <= row) & (lying[:, :seen] == upright)
        bias = jnp.where(allowed, 0.0, -1e30)
        exponents = []
        for head in range(heads):
            masked = scores[i][head * tile : (head + 1) * tile] + bias
            row_max = jnp.max(masked, axis=-1, keepdims=True)
            exponents.append(jnp.exp2((masked - row_max) * factor).astype(jnp.bfloat16))
        values = rows_ref[:seen, 640:768]
        values = jnp.concatenate([values, jnp.ones_like(values)], axis=1)
        context = jnp.dot(
            jnp.concatenate(exponents, axis=0), values, preferred_element_type=jnp.float32
        )
        for head in range(heads):
            part = context[head * tile : (head + 1) * tile]
            result = part[:, :128] / part[:, 128:]
            out_ref[0, here, head * 128 : (head + 1) * 128] = result.astype(jnp.bfloat16)


def attend(where, early, blocks, weights, cosine, sine):
    rows = blocks[0].shape[0]
    total = cosine.shape[0]
    vmem = pl.BlockSpec(memory_space=VMEM)
    flops = 2 * 4 * rows * weights[0].shape[0] * 768
    return pl.pallas_call(
        functools.partial(attend_kernel, where),
        out_shape=jax.ShapeDtypeStruct((1, total, weights[0].shape[1]), jnp.bfloat16),
        in_specs=[vmem] * 10,
        out_specs=vmem,
        scratch_shapes=[pltpu.VMEM((total, 768 + LANES), jnp.bfloat16)],
        compiler_params=pltpu.CompilerParams(vmem_limit_bytes=20 << 20),
        cost_estimate=pl.CostEstimate(flops=flops, bytes_accessed=10 << 20, transcendentals=0),
    )(*early, *blocks, *weights, cosine, sine)


def routes(sections, group):
    def place(section, t):
        return section * group + t % group

    first, second, sibling = [], [], []
    for s in range(sections):
        for t in range(group):
            up = t % 2 == 0
            if s + 1 < sections:
                shift = (2 if up else 0) if s % 2 else (0 if up else -2)
                first.append((place(s, t), place(s + 1, t + shift)))
            second.append((place(s, t), place(s, t + (2 if up else -2))))
            sibling.append((place(s, t), place(s, t ^ 1)))
    return first, second, sibling


def per_device(sections, group, stash, slot, doc_ids, norm_gain, w_query, w_key, value_weight):
    first, second, sibling = routes(sections, group)
    weights = (w_query, w_key, value_weight)

    def go(block, route):
        return lax.ppermute(block, AXES, route)

    where = tuple(
        ((shift, True, swapped), (shift, False, swapped))
        for shift in (0, 1)
        for swapped in (False, True)
    )
    own = normalize(slot, stash, doc_ids, norm_gain)
    near_a = go(own, first)
    other = go(own, sibling)
    near_b = go(other, first)
    cosine, sine = tables(stash.shape[2] * group)
    far_a = go(near_a, second)
    near_c = go(near_a, sibling)
    rows_a = project(where[0], (near_a, near_c), weights, cosine, sine)
    far_b = go(near_b, second)
    near_d = go(near_b, sibling)
    rows_b = project(where[1], (near_b, near_d), weights, cosine, sine)
    far_c = go(far_a, sibling)
    rows_c = project(where[2], (far_a, far_c), weights, cosine, sine)
    far_d = go(far_b, sibling)
    early = (rows_a, rows_b, rows_c)
    return attend(where, early, (far_b, far_d), weights, cosine, sine)


def solution(mesh):
    placed = (
        P("section", None, "tp", None),
        P("section"),
        P("section", None, "tp"),
        P(),
        P(None, "tp"),
        P(None, "tp"),
        P(None, "tp"),
    )
    return jax.shard_map(
        functools.partial(per_device, mesh.shape["section"], mesh.shape["tp"]),
        mesh=mesh,
        in_specs=placed,
        out_specs=P("section", None, "tp"),
        check_vma=False,
    )
```

profile of v0, /device:TPU:127, one launch (start us, length us, event | category | flops | bytes accessed | tf_op | source)
XLA Modules:
  0.0 85.8 jit_solution(580428166568174268)
XLA Ops:
  0.7 0.0 copy-start.3
  0.7 1.7 %shard_map.82 = bf16[64,4224]{1,0:T(8,128)(2,1)S(1)} custom-call(s32[1]{0:T(128)S(6)} %copy.9.slot_ref, bf16[1,2,64,4096]{3,2,1,0:T(8,128)(2,1)} %stash_ref.1, s32[1,2,64]{2,1,0:T(2,128)} %doc_ref.1, bf16[32,128]{1,0:T(8,128)(2,1)} %bitcast.1), custom_call_target="tpu_custom_call" | custom-call | tf_op jit(solution)/shard_map/pallas_call | solution.py:67
  2.3 2.6 %collective-permute-start.2 = (bf16[64,4224]{1,0:T(8,128)(2,1)S(1)}, bf16[64,4224]{1,0:T(8,128)(2,1)S(1)}, u32[]{:S(2)}, u32[]{:S(2)}) collective-permute-start(bf16[64,4224]{1,0:T(8,128)(2,1)S(1)} %shard_map.82), channel_id=1, source_target_pairs={{0,1},{1,0},{2,3},{3,2},{4,5},{5,4},{6,7},{7,6},{8,9},{9,8},{10,11... | collective-permute-start | bytes 1622024 | tf_op jit(solution)/shard_map/ppermute | solution.py:257
  4.9 17.0 %collective-permute-start = (bf16[64,4224]{1,0:T(8,128)(2,1)S(1)}, bf16[64,4224]{1,0:T(8,128)(2,1)S(1)}, u32[]{:S(2)}, u32[]{:S(2)}) collective-permute-start(bf16[64,4224]{1,0:T(8,128)(2,1)S(1)} %shard_map.82), channel_id=1, source_target_pairs={{0,8},{1,15},{2,10},{3,9},{4,12},{5,11},{6,14},{7,13},{8,18},{9,17... | collective-permute-start | bytes 1622024 | tf_op jit(solution)/shard_map/ppermute | solution.py:257
  22.0 0.0 collective-permute-done.2
  22.0 1.9 %collective-permute-start.3 = (bf16[64,4224]{1,0:T(8,128)(2,1)S(1)}, bf16[64,4224]{1,0:T(8,128)(2,1)S(1)}, u32[]{:S(2)}, u32[]{:S(2)}) collective-permute-start(bf16[64,4224]{1,0:T(8,128)(2,1)S(1)} %collective-permute-done.2), channel_id=1, source_target_pairs={{0,8},{1,15},{2,10},{3,9},{4,12},{5,11},{6,14},{7,13},{8,18},{9,17... | collective-permute-start | bytes 1622024 | tf_op jit(solution)/shard_map/ppermute | solution.py:257
  23.9 4.3 %collective-permute-done.b0 = bf16[64,4224]{1,0:T(8,128)(2,1)S(1)} collective-permute-done((bf16[64,4224]{1,0:T(8,128)(2,1)S(1)}, bf16[64,4224]{1,0:T(8,128)(2,1)S(1)}, u32[]{:S(2)}, u32[]{:S(2)}) %collective-permute-start) | collective-permute-done | bytes 540704 | tf_op jit(solution)/shard_map/ppermute | solution.py:257
  28.3 10.3 %collective-permute-start.5 = (bf16[64,4224]{1,0:T(8,128)(2,1)S(1)}, bf16[64,4224]{1,0:T(8,128)(2,1)S(1)}, u32[]{:S(2)}, u32[]{:S(2)}) collective-permute-start(bf16[64,4224]{1,0:T(8,128)(2,1)S(1)} %collective-permute-done.b0), channel_id=1, source_target_pairs={{0,2},{1,7},{2,4},{3,1},{4,6},{5,3},{6,0},{7,5},{8,10},{9,15},{10,... | collective-permute-start | bytes 1622024 | tf_op jit(solution)/shard_map/ppermute | solution.py:257
  38.6 0.0 collective-permute-done.3.b0
  38.6 11.8 %collective-permute-start.7 = (bf16[64,4224]{1,0:T(8,128)(2,1)S(1)}, bf16[64,4224]{1,0:T(8,128)(2,1)S(1)}, u32[]{:S(2)}, u32[]{:S(2)}) collective-permute-start(bf16[64,4224]{1,0:T(8,128)(2,1)S(1)} %collective-permute-done.3.b0), channel_id=1, source_target_pairs={{0,2},{1,7},{2,4},{3,1},{4,6},{5,3},{6,0},{7,5},{8,10},{9,15},{10,... | collective-permute-start | bytes 1622024 | tf_op jit(solution)/shard_map/ppermute | solution.py:257
  50.4 2.0 %collective-permute-start.1 = (bf16[64,4224]{1,0:T(8,128)(2,1)S(1)}, bf16[64,4224]{1,0:T(8,128)(2,1)S(1)}, u32[]{:S(2)}, u32[]{:S(2)}) collective-permute-start(bf16[64,4224]{1,0:T(8,128)(2,1)S(1)} %collective-permute-done.b0), channel_id=1, source_target_pairs={{0,1},{1,0},{2,3},{3,2},{4,5},{5,4},{6,7},{7,6},{8,9},{9,8},{10,11... | collective-permute-start | bytes 1622024 | tf_op jit(solution)/shard_map/ppermute | solution.py:257
  52.4 2.3 %collective-permute-start.4 = (bf16[64,4224]{1,0:T(8,128)(2,1)S(1)}, bf16[64,4224]{1,0:T(8,128)(2,1)S(1)}, u32[]{:S(2)}, u32[]{:S(2)}) collective-permute-start(bf16[64,4224]{1,0:T(8,128)(2,1)S(1)} %collective-permute-done.3.b0), channel_id=1, source_target_pairs={{0,1},{1,0},{2,3},{3,2},{4,5},{5,4},{6,7},{7,6},{8,9},{9,8},{10,11... | collective-permute-start | bytes 1622024 | tf_op jit(solution)/shard_map/ppermute | solution.py:257
  54.7 0.0 collective-permute-done.5.b0
  54.8 2.0 %collective-permute-start.6 = (bf16[64,4224]{1,0:T(8,128)(2,1)S(1)}, bf16[64,4224]{1,0:T(8,128)(2,1)S(1)}, u32[]{:S(2)}, u32[]{:S(2)}) collective-permute-start(bf16[64,4224]{1,0:T(8,128)(2,1)S(1)} %collective-permute-done.5.b0), channel_id=1, source_target_pairs={{0,1},{1,0},{2,3},{3,2},{4,5},{5,4},{6,7},{7,6},{8,9},{9,8},{10,11... | collective-permute-start | bytes 1622024 | tf_op jit(solution)/shard_map/ppermute | solution.py:257
  56.7 3.9 %collective-permute-done.7.b0 = bf16[64,4224]{1,0:T(8,128)(2,1)S(1)} collective-permute-done((bf16[64,4224]{1,0:T(8,128)(2,1)S(1)}, bf16[64,4224]{1,0:T(8,128)(2,1)S(1)}, u32[]{:S(2)}, u32[]{:S(2)}) %collective-permute-start.7) | collective-permute-done | bytes 540704 | tf_op jit(solution)/shard_map/ppermute | solution.py:257
  60.7 10.8 %collective-permute-start.8 = (bf16[64,4224]{1,0:T(8,128)(2,1)S(1)}, bf16[64,4224]{1,0:T(8,128)(2,1)S(1)}, u32[]{:S(2)}, u32[]{:S(2)}) collective-permute-start(bf16[64,4224]{1,0:T(8,128)(2,1)S(1)} %collective-permute-done.7.b0), channel_id=1, source_target_pairs={{0,1},{1,0},{2,3},{3,2},{4,5},{5,4},{6,7},{7,6},{8,9},{9,8},{10,11... | collective-permute-start | bytes 1622024 | tf_op jit(solution)/shard_map/ppermute | solution.py:257
  71.5 0.0 copy-start.6
  71.5 0.6 copy-done.6
  72.1 1.0 %shard_map.83 = (f32[512,128]{1,0:T(8,128)S(1)}, f32[512,128]{1,0:T(8,128)S(1)}) custom-call(f32[1,128]{1,0:T(1,128)S(1)} %copy-done.6), custom_call_target="tpu_custom_call" | custom-call | flops 4194304 | bytes 1048576 | tf_op jit(solution)/shard_map/pallas_call | solution.py:97
  73.1 0.0 collective-permute-done.1.b1
  73.1 0.0 copy-start
  73.1 2.2 %copy-done = bf16[4096,512]{1,0:T(8,128)(2,1)S(1)} copy-done((bf16[4096,512]{1,0:T(8,128)(2,1)S(1)}, bf16[4096,512]{1,0:T(8,128)(2,1)}, u32[]{:S(2)}) %copy-start) | copy-done | bytes 4194328
  75.3 0.0 copy-start.2
  75.3 1.2 %copy-done.2 = bf16[4096,128]{1,0:T(8,128)(2,1)S(1)} copy-done((bf16[4096,128]{1,0:T(8,128)(2,1)S(1)}, bf16[4096,128]{1,0:T(8,128)(2,1)}, u32[]{:S(2)}) %copy-start.2) | copy-done | bytes 1048600
  76.5 0.0 copy-start.4
  76.5 1.2 %copy-done.4 = bf16[4096,128]{1,0:T(8,128)(2,1)S(1)} copy-done((bf16[4096,128]{1,0:T(8,128)(2,1)S(1)}, bf16[4096,128]{1,0:T(8,128)(2,1)}, u32[]{:S(2)}) %copy-start.4) | copy-done | bytes 1048600
  77.7 0.0 copy-start.1
  77.7 0.0 copy-start.5
  77.7 1.1 %shard_map.84.e0 = bf16[128,896]{1,0:T(8,128)(2,1)S(1)} custom-call(bf16[64,4224]{1,0:T(8,128)(2,1)S(1)} %collective-permute-done.b0, bf16[64,4224]{1,0:T(8,128)(2,1)S(1)} %collective-permute-done.1.b1, bf16[4096,512]{1,0:T(8,128)(2,1)S(1)} %copy-done, bf16[4096,128]{1,0:T(8,128)(2,1)S(1)} %copy-done.2, bf16[4096,128]{1,0:T(8,128)(2,1)S(1)} %copy-done.4, ...), custom_call_target="tpu_custom_call" | custom-call | flops 805306368 | bytes 8388608 | tf_op jit(solution)/shard_map/pallas_call | solution.py:151
  78.8 0.0 collective-permute-done.4.b1
  78.8 0.0 copy-done.3
  78.8 1.1 %copy-done.1 = bf16[4096,512]{1,0:T(8,128)(2,1)S(1)} copy-done((bf16[4096,512]{1,0:T(8,128)(2,1)S(1)}, bf16[4096,512]{1,0:T(8,128)(2,1)}, u32[]{:S(2)}) %copy-start.1) | copy-done | bytes 4194328
  79.9 0.3 copy-done.5
  80.2 1.1 %shard_map.85.e1 = bf16[128,896]{1,0:T(8,128)(2,1)S(1)} custom-call(bf16[64,4224]{1,0:T(8,128)(2,1)S(1)} %collective-permute-done.3.b0, bf16[64,4224]{1,0:T(8,128)(2,1)S(1)} %collective-permute-done.4.b1, bf16[4096,512]{1,0:T(8,128)(2,1)S(1)} %copy-done.1, bf16[4096,128]{1,0:T(8,128)(2,1)S(1)} %copy-done.3, bf16[4096,128]{1,0:T(8,128)(2,1)S(1)} %copy-done.5, ...), custom_call_target="tpu_custom_call" | custom-call | flops 805306368 | bytes 8388608 | tf_op jit(solution)/shard_map/pallas_call | solution.py:151
  81.3 0.0 collective-permute-done.6.b1
  81.3 1.1 %shard_map.86.e2 = bf16[128,896]{1,0:T(8,128)(2,1)S(1)} custom-call(bf16[64,4224]{1,0:T(8,128)(2,1)S(1)} %collective-permute-done.5.b0, bf16[64,4224]{1,0:T(8,128)(2,1)S(1)} %collective-permute-done.6.b1, bf16[4096,512]{1,0:T(8,128)(2,1)S(1)} %copy-done.1, bf16[4096,128]{1,0:T(8,128)(2,1)S(1)} %copy-done.3, bf16[4096,128]{1,0:T(8,128)(2,1)S(1)} %copy-done.5, ...), custom_call_target="tpu_custom_call" | custom-call | flops 805306368 | bytes 8388608 | tf_op jit(solution)/shard_map/pallas_call | solution.py:151
  82.4 0.0 collective-permute-done.8.b1
  82.4 3.4 %shard_map.87 = bf16[1,512,512]{2,1,0:T(8,128)(2,1)} custom-call(bf16[128,896]{1,0:T(8,128)(2,1)S(1)} %shard_map.84.e0, bf16[128,896]{1,0:T(8,128)(2,1)S(1)} %shard_map.85.e1, bf16[128,896]{1,0:T(8,128)(2,1)S(1)} %shard_map.86.e2, bf16[64,4224]{1,0:T(8,128)(2,1)S(1)} %collective-permute-done.7.b0, bf16[64,4224]{1,0:T(8,128)(2,1)S(1)} %collective-permute-done.8.b1, ...), custom_call_target="tpu_custom_call" | custom-call | flops 1610612736 | bytes 10485760 | tf_op jit(solution)/shard_map/pallas_call | solution.py:225
Async XLA Ops:
  0.7 78.2 %copy-start.3 = (bf16[4096,128]{1,0:T(8,128)(2,1)S(1)}, bf16[4096,128]{1,0:T(8,128)(2,1)}, u32[]{:S(2)}) copy-start(bf16[4096,128]{1,0:T(8,128)(2,1)} %w_key.7) | copy-start | bytes 3145732
  2.3 19.6 %collective-permute-start.2 = (bf16[64,4224]{1,0:T(8,128)(2,1)S(1)}, bf16[64,4224]{1,0:T(8,128)(2,1)S(1)}, u32[]{:S(2)}, u32[]{:S(2)}) collective-permute-start(bf16[64,4224]{1,0:T(8,128)(2,1)S(1)} %shard_map.82), channel_id=1, source_target_pairs={{0,1},{1,0},{2,3},{3,2},{4,5},{5,4},{6,7},{7,6},{8,9},{9,8},{10,11... | collective-permute-start | bytes 1622024 | tf_op jit(solution)/shard_map/ppermute | solution.py:257
  4.9 23.3 %collective-permute-start = (bf16[64,4224]{1,0:T(8,128)(2,1)S(1)}, bf16[64,4224]{1,0:T(8,128)(2,1)S(1)}, u32[]{:S(2)}, u32[]{:S(2)}) collective-permute-start(bf16[64,4224]{1,0:T(8,128)(2,1)S(1)} %shard_map.82), channel_id=1, source_target_pairs={{0,8},{1,15},{2,10},{3,9},{4,12},{5,11},{6,14},{7,13},{8,18},{9,17... | collective-permute-start | bytes 1622024 | tf_op jit(solution)/shard_map/ppermute | solution.py:257
  22.0 16.6 %collective-permute-start.3 = (bf16[64,4224]{1,0:T(8,128)(2,1)S(1)}, bf16[64,4224]{1,0:T(8,128)(2,1)S(1)}, u32[]{:S(2)}, u32[]{:S(2)}) collective-permute-start(bf16[64,4224]{1,0:T(8,128)(2,1)S(1)} %collective-permute-done.2), channel_id=1, source_target_pairs={{0,8},{1,15},{2,10},{3,9},{4,12},{5,11},{6,14},{7,13},{8,18},{9,17... | collective-permute-start | bytes 1622024 | tf_op jit(solution)/shard_map/ppermute | solution.py:257
  28.3 26.5 %collective-permute-start.5 = (bf16[64,4224]{1,0:T(8,128)(2,1)S(1)}, bf16[64,4224]{1,0:T(8,128)(2,1)S(1)}, u32[]{:S(2)}, u32[]{:S(2)}) collective-permute-start(bf16[64,4224]{1,0:T(8,128)(2,1)S(1)} %collective-permute-done.b0), channel_id=1, source_target_pairs={{0,2},{1,7},{2,4},{3,1},{4,6},{5,3},{6,0},{7,5},{8,10},{9,15},{10,... | collective-permute-start | bytes 1622024 | tf_op jit(solution)/shard_map/ppermute | solution.py:257
  38.6 22.1 %collective-permute-start.7 = (bf16[64,4224]{1,0:T(8,128)(2,1)S(1)}, bf16[64,4224]{1,0:T(8,128)(2,1)S(1)}, u32[]{:S(2)}, u32[]{:S(2)}) collective-permute-start(bf16[64,4224]{1,0:T(8,128)(2,1)S(1)} %collective-permute-done.3.b0), channel_id=1, source_target_pairs={{0,2},{1,7},{2,4},{3,1},{4,6},{5,3},{6,0},{7,5},{8,10},{9,15},{10,... | collective-permute-start | bytes 1622024 | tf_op jit(solution)/shard_map/ppermute | solution.py:257
  50.4 22.7 %collective-permute-start.1 = (bf16[64,4224]{1,0:T(8,128)(2,1)S(1)}, bf16[64,4224]{1,0:T(8,128)(2,1)S(1)}, u32[]{:S(2)}, u32[]{:S(2)}) collective-permute-start(bf16[64,4224]{1,0:T(8,128)(2,1)S(1)} %collective-permute-done.b0), channel_id=1, source_target_pairs={{0,1},{1,0},{2,3},{3,2},{4,5},{5,4},{6,7},{7,6},{8,9},{9,8},{10,11... | collective-permute-start | bytes 1622024 | tf_op jit(solution)/shard_map/ppermute | solution.py:257
  52.4 26.4 %collective-permute-start.4 = (bf16[64,4224]{1,0:T(8,128)(2,1)S(1)}, bf16[64,4224]{1,0:T(8,128)(2,1)S(1)}, u32[]{:S(2)}, u32[]{:S(2)}) collective-permute-start(bf16[64,4224]{1,0:T(8,128)(2,1)S(1)} %collective-permute-done.3.b0), channel_id=1, source_target_pairs={{0,1},{1,0},{2,3},{3,2},{4,5},{5,4},{6,7},{7,6},{8,9},{9,8},{10,11... | collective-permute-start | bytes 1622024 | tf_op jit(solution)/shard_map/ppermute | solution.py:257
  54.8 26.5 %collective-permute-start.6 = (bf16[64,4224]{1,0:T(8,128)(2,1)S(1)}, bf16[64,4224]{1,0:T(8,128)(2,1)S(1)}, u32[]{:S(2)}, u32[]{:S(2)}) collective-permute-start(bf16[64,4224]{1,0:T(8,128)(2,1)S(1)} %collective-permute-done.5.b0), channel_id=1, source_target_pairs={{0,1},{1,0},{2,3},{3,2},{4,5},{5,4},{6,7},{7,6},{8,9},{9,8},{10,11... | collective-permute-start | bytes 1622024 | tf_op jit(solution)/shard_map/ppermute | solution.py:257
  60.7 21.7 %collective-permute-start.8 = (bf16[64,4224]{1,0:T(8,128)(2,1)S(1)}, bf16[64,4224]{1,0:T(8,128)(2,1)S(1)}, u32[]{:S(2)}, u32[]{:S(2)}) collective-permute-start(bf16[64,4224]{1,0:T(8,128)(2,1)S(1)} %collective-permute-done.7.b0), channel_id=1, source_target_pairs={{0,1},{1,0},{2,3},{3,2},{4,5},{5,4},{6,7},{7,6},{8,9},{9,8},{10,11... | collective-permute-start | bytes 1622024 | tf_op jit(solution)/shard_map/ppermute | solution.py:257
  71.5 0.7 copy-start.6
  73.1 2.2 %copy-start = (bf16[4096,512]{1,0:T(8,128)(2,1)S(1)}, bf16[4096,512]{1,0:T(8,128)(2,1)}, u32[]{:S(2)}) copy-start(bf16[4096,512]{1,0:T(8,128)(2,1)} %w_query.7) | copy-start | bytes 12582916
  75.3 1.2 %copy-start.2 = (bf16[4096,128]{1,0:T(8,128)(2,1)S(1)}, bf16[4096,128]{1,0:T(8,128)(2,1)}, u32[]{:S(2)}) copy-start(bf16[4096,128]{1,0:T(8,128)(2,1)} %w_key.7) | copy-start | bytes 3145732
  76.5 1.2 %copy-start.4 = (bf16[4096,128]{1,0:T(8,128)(2,1)S(1)}, bf16[4096,128]{1,0:T(8,128)(2,1)}, u32[]{:S(2)}) copy-start(bf16[4096,128]{1,0:T(8,128)(2,1)} %w_value.7) | copy-start | bytes 3145732
  77.7 2.2 %copy-start.1 = (bf16[4096,512]{1,0:T(8,128)(2,1)S(1)}, bf16[4096,512]{1,0:T(8,128)(2,1)}, u32[]{:S(2)}) copy-start(bf16[4096,512]{1,0:T(8,128)(2,1)} %w_query.7) | copy-start | bytes 12582916
  77.7 2.5 %copy-start.5 = (bf16[4096,128]{1,0:T(8,128)(2,1)S(1)}, bf16[4096,128]{1,0:T(8,128)(2,1)}, u32[]{:S(2)}) copy-start(bf16[4096,128]{1,0:T(8,128)(2,1)} %w_value.7) | copy-start | bytes 3145732
where the time goes:
time: 86.3 us; the launch traced here: 85.8 us
  starting transfers between devices  60.7 us (70%)
  Pallas kernels  9.28 us (11%)
  waiting for transfers between devices  8.3 us (10%)
  local copies, waits for them, and re-layouts  6.68 us (8%)
    ppermute x9, starting transfers between devices, go(): return lax.ppermute(block, AXES, route)  60.7 us
    ppermute x9, waiting for transfers between devices, go(): return lax.ppermute(block, AXES, route)  8.3 us
    unnamed x14, local copies, waits for them, and re-layouts  6.68 us
    pallas_call x1, Pallas kernels, attend(): pl.pallas_call(functools.partial(attend_kernel, where), out_shape=jax.Sha...  3.44 us
    pallas_call x3, Pallas kernels, project(): pl.pallas_call(functools.partial(project_kernel, where), out_shape=jax.Sh...  3.21 us
  transfers between devices with their start and end apart: 9, of which 2 were waited for; matrix products, arithmetic and copies ran while one was open for 0% of the time, Pallas kernels for 5%

commit v1 on v0

v1 whole, which is shorter than its diff:
```python
import functools
import math

import jax
import jax.numpy as jnp
import numpy as np
from jax import lax
from jax.experimental import pallas as pl
from jax.experimental.pallas import tpu as pltpu
from jax.sharding import PartitionSpec as P

HEAD_SIZE = 128
LANES = 128
ROPE_BASE = 500000.0
NORM_EPSILON = 1e-05
AXES = ("section", "tp")
VMEM = pltpu.MemorySpace.VMEM


def fetch(source, target, sem):
    return pltpu.make_async_copy(source, target, sem)


def stay(x):
    return pltpu.with_memory_space_constraint(x, pltpu.MemorySpace.HBM)


def normalize_kernel(
    slot_ref, stash_ref, doc_ref, gain_ref, out_ref, low, high, docs, gain_buf, buf, sems
):
    rows, width = buf.shape
    pieces = sems.shape[0] - 2
    step = rows // pieces
    pick = slot_ref[0]
    copies = [
        fetch(doc_ref, docs, sems.at[0]),
        fetch(gain_ref, gain_buf, sems.at[1]),
    ]
    for i in range(pieces):
        part = pl.ds(i * step, step)
        copies.append(fetch(stash_ref.at[0, pick, part], buf.at[part], sems.at[2 + i]))
    for copy in copies:
        copy.start()
    for copy in copies[:2]:
        copy.wait()
    numbers = docs[0, pl.ds(pick, 1), :].astype(jnp.float32)
    row = lax.broadcasted_iota(jnp.int32, (rows, rows), 0)
    column = lax.broadcasted_iota(jnp.int32, (rows, rows), 1)
    upright = jnp.sum(jnp.where(row == column, numbers, 0.0), axis=1, keepdims=True)
    upright = jnp.broadcast_to(upright, (rows, LANES)).astype(jnp.bfloat16)
    out_ref[:, width:] = upright
    low[:, width:] = upright[: rows // 2]
    high[:, width:] = upright[rows // 2 :]
    gain = gain_buf[...].astype(jnp.float32)
    for i in range(pieces):
        copies[2 + i].wait()
        part = slice(i * step, (i + 1) * step)
        x = buf[part, :].astype(jnp.float32)
        scale = lax.rsqrt(jnp.mean(x * x, axis=-1, keepdims=True) + NORM_EPSILON)
        for j in range(width // LANES):
            lanes = slice(j * LANES, (j + 1) * LANES)
            scaled = (x[:, lanes] * scale * gain[j : j + 1, :]).astype(jnp.bfloat16)
            out_ref[part, lanes] = scaled
            first = i * step % (rows // 2)
            piece = low if i < pieces // 2 else high
            piece[first : first + step, lanes] = scaled


def normalize(slot, stash, doc_ids, gain):
    rows, width = stash.shape[2:]
    pieces = 4
    hbm = pl.BlockSpec(memory_space=pltpu.MemorySpace.HBM)

    return pl.pallas_call(
        normalize_kernel,
        out_shape=[
            jax.ShapeDtypeStruct((count, width + LANES), jnp.bfloat16)
            for count in (rows, rows // 2, rows // 2)
        ],
        in_specs=[pl.BlockSpec(memory_space=pltpu.MemorySpace.SMEM)] + [hbm] * 3,
        out_specs=[pl.BlockSpec(memory_space=VMEM)] * 3,
        scratch_shapes=[
            pltpu.VMEM(doc_ids.shape, doc_ids.dtype),
            pltpu.VMEM((width // LANES, LANES), gain.dtype),
            pltpu.VMEM((rows, width), jnp.bfloat16),
            pltpu.SemaphoreType.DMA((2 + pieces,)),
        ],
        compiler_params=pltpu.CompilerParams(vmem_limit_bytes=8 << 20),
    )(slot, stay(stash), stay(doc_ids), stay(gain.reshape(-1, LANES)))


def prepare_kernel(inverse_ref, w_query, w_key, w_value, cosine, sine, weights, sems):
    start, copies = 0, []
    for index, part in enumerate((w_query, w_key, w_value)):
        columns = part.shape[1]
        copies.append(fetch(part, weights.at[:, pl.ds(start, columns)], sems.at[index]))
        start += columns
    for copy in copies:
        copy.start()
    rows = cosine.shape[0]
    position = lax.broadcasted_iota(jnp.int32, (rows, LANES), 0).astype(jnp.float32)
    lane = lax.broadcasted_iota(jnp.int32, (rows, LANES), 1)
    angle = position * inverse_ref[...]
    cosine[...] = jnp.cos(angle)
    turned = jnp.sin(angle)
    sine[...] = jnp.where(lane < HEAD_SIZE // 2, -turned, turned)
    for copy in copies:
        copy.wait()


def prepare(total, w_query, w_key, w_value):
    exponent = -2.0 * np.arange(HEAD_SIZE // 2) / HEAD_SIZE
    inverse = np.tile(ROPE_BASE**exponent, 2)[None].astype(np.float32)
    parts = (w_query, w_key, w_value)
    vmem = pl.BlockSpec(memory_space=VMEM)
    hbm = pl.BlockSpec(memory_space=pltpu.MemorySpace.HBM)
    shape = jax.ShapeDtypeStruct((total, LANES), jnp.float32)
    columns = sum(part.shape[1] for part in parts)
    return pl.pallas_call(
        prepare_kernel,
        out_shape=(
            shape,
            shape,
            jax.ShapeDtypeStruct((w_query.shape[0], columns), w_query.dtype),
        ),
        in_specs=[vmem] + [hbm] * 3,
        out_specs=(vmem,) * 3,
        scratch_shapes=[pltpu.SemaphoreType.DMA((3,))],
        compiler_params=pltpu.CompilerParams(vmem_limit_bytes=10 << 20),
        cost_estimate=pl.CostEstimate(flops=4 << 20, bytes_accessed=8 << 20, transcendentals=0),
    )(inverse, *[stay(part) for part in parts])


def granule(chip_shift, mine, swapped):
    t, odd = lax.axis_index("tp"), 1 - lax.axis_index("section") % 2
    core, chips = t % 2, lax.axis_size("tp") // 2
    up = core if mine else 1 - core
    chip = lax.rem(t // 2 - odd + chips + jnp.where(up == 0, -chip_shift, 1 + chip_shift), chips)
    return 2 * chip + (1 - up if swapped else up)


def row_of(place, rows):
    return pl.multiple_of(granule(*place[:3]) * rows + place[3], 16)


def project_to(blocks, places, weights, cosine, sine, rows, store):
    width = weights.shape[0]
    x = jnp.concatenate([block[:, :width] for block in blocks], axis=0)
    numbers = jnp.concatenate([block[:, width:] for block in blocks], axis=0)
    products = [
        jnp.dot(x, weights[:, start : start + 256], preferred_element_type=jnp.float32)
        for start in range(0, 768, 256)
    ]
    first = 0
    for place in places:
        count, position = place[4], row_of(place, rows)
        here = slice(first, first + count)
        cos, sin = cosine[pl.ds(position, count), :], sine[pl.ds(position, count), :]
        for head in range(6):
            values = products[head // 2][here, (head % 2) * 128 : (head % 2) * 128 + 128]
            if head < 5:
                values = values * cos + pltpu.roll(values, 64, 1) * sin
            store(here, pl.ds(position, count), head * 128, values.astype(jnp.bfloat16))
        store(here, pl.ds(position, count), 768, numbers[here])
        first += count


def project_kernel(places, rows, b0, b1, weights, cosine, sine, out_ref):
    def store(here, there, column, values):
        out_ref[here, column : column + 128] = values

    project_to((b0, b1), places, weights, cosine, sine, rows, store)


def project(places, rows, blocks, weights, cosine, sine):
    count = sum(place[4] for place in places)
    vmem = pl.BlockSpec(memory_space=VMEM)
    flops = 2 * count * weights.shape[0] * 768
    return pl.pallas_call(
        functools.partial(project_kernel, places, rows),
        out_shape=jax.ShapeDtypeStruct((count, 768 + LANES), jnp.bfloat16),
        in_specs=[vmem] * 5,
        out_specs=vmem,
        compiler_params=pltpu.CompilerParams(vmem_limit_bytes=16 << 20),
        cost_estimate=pl.CostEstimate(flops=flops, bytes_accessed=8 << 20, transcendentals=0),
    )(*blocks, weights, cosine, sine)


def attend_kernel(
    near, far, last, rows, e0, e1, b0, b1, weights, cosine, sine, out_ref, rows_ref
):
    def store(here, there, column, values):
        rows_ref[there, column : column + 128] = values

    for places, early in ((near, e0), (far, e1)):
        first = 0
        for place in places:
            count = place[4]
            rows_ref[pl.ds(row_of(place, rows), count), :] = early[first : first + count, :]
            first += count
    project_to((b0, b1), last, weights, cosine, sine, rows, store)

    total = rows_ref.shape[0]
    heads, tile = 4, 128
    factor = math.log2(math.e) / math.sqrt(HEAD_SIZE)
    contract_last = (((1,), (1,)), ((), ()))
    ones = jnp.ones((8, LANES), jnp.bfloat16)
    lying = lax.dot_general(
        ones, rows_ref[:, 768:], contract_last, preferred_element_type=jnp.float32
    )[:1, :]
    scores = []
    for i in range(total // tile):
        here = slice(i * tile, (i + 1) * tile)
        queries = [rows_ref[here, h * 128 : (h + 1) * 128] for h in range(heads)]
        scores.append(
            lax.dot_general(
                jnp.concatenate(queries, axis=0),
                rows_ref[: (i + 1) * tile, 512:640],
                contract_last,
                preferred_element_type=jnp.float32,
            )
        )
    for i in range(total // tile):
        seen = (i + 1) * tile
        here = slice(i * tile, seen)
        upright = rows_ref[here, 768:769].astype(jnp.float32) * float(LANES)
        row = lax.broadcasted_iota(jnp.int32, (tile, seen), 0) + i * tile
        column = lax.broadcasted_iota(jnp.int32, (tile, seen), 1)
        allowed = (column <= row) & (lying[:, :seen] == upright)
        bias = jnp.where(allowed, 0.0, -1e30)
        exponents = []
        for head in range(heads):
            masked = scores[i][head * tile : (head + 1) * tile] + bias
            row_max = jnp.max(masked, axis=-1, keepdims=True)
            exponents.append(jnp.exp2((masked - row_max) * factor).astype(jnp.bfloat16))
        values = rows_ref[:seen, 640:768]
        values = jnp.concatenate([values, jnp.ones_like(values)], axis=1)
        context = jnp.dot(
            jnp.concatenate(exponents, axis=0), values, preferred_element_type=jnp.float32
        )
        for head in range(heads):
            part = context[head * tile : (head + 1) * tile]
            result = part[:, :128] / part[:, 128:]
            out_ref[0, here, head * 128 : (head + 1) * 128] = result.astype(jnp.bfloat16)


def attend(near, far, last, rows, early, blocks, weights, cosine, sine):
    total = cosine.shape[0]
    vmem = pl.BlockSpec(memory_space=VMEM)
    flops = 4 * total * total * 512
    return pl.pallas_call(
        functools.partial(attend_kernel, near, far, last, rows),
        out_shape=jax.ShapeDtypeStruct((1, total, 512), jnp.bfloat16),
        in_specs=[vmem] * 7,
        out_specs=vmem,
        scratch_shapes=[pltpu.VMEM((total, 768 + LANES), jnp.bfloat16)],
        compiler_params=pltpu.CompilerParams(vmem_limit_bytes=20 << 20),
        cost_estimate=pl.CostEstimate(flops=flops, bytes_accessed=10 << 20, transcendentals=0),
    )(*early, *blocks, weights, cosine, sine)


def join_kernel(*refs):
    first = 0
    for block in refs[:-1]:
        count = block.shape[0]
        refs[-1][first : first + count, :] = block[...]
        first += count


def join(*blocks):
    vmem = pl.BlockSpec(memory_space=VMEM)
    rows, width = sum(block.shape[0] for block in blocks), blocks[0].shape[1]
    return pl.pallas_call(
        join_kernel,
        out_shape=jax.ShapeDtypeStruct((rows, width), blocks[0].dtype),
        in_specs=[vmem] * len(blocks),
        out_specs=vmem,
        compiler_params=pltpu.CompilerParams(vmem_limit_bytes=6 << 20),
        cost_estimate=pl.CostEstimate(flops=1 << 20, bytes_accessed=1 << 20, transcendentals=0),
    )(*blocks)


def routes(sections, group):
    def place(section, t):
        return section * group + t % group

    first, second, sibling = [], [], []
    for s in range(sections):
        for t in range(group):
            up = t % 2 == 0
            if s + 1 < sections:
                shift = (2 if up else 0) if s % 2 else (0 if up else -2)
                first.append((place(s, t), place(s + 1, t + shift)))
            second.append((place(s, t), place(s, t + (2 if up else -2))))
            sibling.append((place(s, t), place(s, t ^ 1)))
    return first, second, sibling


def per_device(sections, group, stash, slot, doc_ids, norm_gain, w_query, w_key, value_weight):
    first, second, sibling = routes(sections, group)

    def go(block, route):
        return lax.ppermute(block, AXES, route)

    rows = stash.shape[2]

    def places(shift, parts):
        return [(shift, mine, *part) for mine in (True, False) for part in parts]

    near_places = places(0, [(False, 0, rows), (True, 0, rows)])
    far_places = places(1, [(False, 0, rows)])
    last_places = places(1, [(True, 0, rows)])
    own, low, high = normalize(slot, stash, doc_ids, norm_gain)
    near_a = go(low, first)
    near_b = go(high, first)
    other = go(own, sibling)
    near_c = go(other, first)
    cosine, sine, weights = prepare(rows * group, w_query, w_key, value_weight)
    far_a = go(near_a, second)
    far_b = go(near_b, second)
    far_c = go(near_c, second)
    near = join(near_a, near_b, near_c)
    near_other = go(near, sibling)
    far = join(far_a, far_b)
    far_other = go(far, sibling)
    rows_near = project(near_places, rows, (near, near_other), weights, cosine, sine)
    rows_far = project(far_places, rows, (far, far_other), weights, cosine, sine)
    last_other = go(far_c, sibling)
    return attend(
        near_places,
        far_places,
        last_places,
        rows,
        (rows_near, rows_far),
        (far_c, last_other),
        weights,
        cosine,
        sine,
    )


def solution(mesh):
    placed = (
        P("section", None, "tp", None),
        P("section"),
        P("section", None, "tp"),
        P(),
        P(None, "tp"),
        P(None, "tp"),
        P(None, "tp"),
    )
    return jax.shard_map(
        functools.partial(per_device, mesh.shape["section"], mesh.shape["tp"]),
        mesh=mesh,
        in_specs=placed,
        out_specs=P("section", None, "tp"),
        check_vma=False,
    )
```

time: 86.3 us -> 94.1 us (1.090)
  the two profiles are of different devices: /device:TPU:127 before, /device:TPU:63 now
where the time goes in v1:
time: 94.1 us; the launch traced here: 93.7 us
  starting transfers between devices  54.3 us (58%)
  waiting for transfers between devices  27.6 us (29%)
  Pallas kernels  10.9 us (12%)
    ppermute x10, starting transfers between devices, go(): return lax.ppermute(block, AXES, route)  54.3 us
    ppermute x10, waiting for transfers between devices, go(): return lax.ppermute(block, AXES, route)  27.6 us
    pallas_call x1, Pallas kernels, attend(): pl.pallas_call(functools.partial(attend_kernel, near, far, last, rows), o...  3.43 us
    pallas_call x2, Pallas kernels, project(): pl.pallas_call(functools.partial(project_kernel, places, rows), out_shape...  2.96 us
    pallas_call x1, Pallas kernels, prepare(): pl.pallas_call(prepare_kernel, out_shape=(shape, shape, jax.ShapeDtypeStr...  2.83 us
  transfers between devices with their start and end apart: 10, of which 5 were waited for; matrix products, arithmetic and copies ran while one was open for 0% of the time, Pallas kernels for 6%

profile of v1, /device:TPU:63, one launch (start us, length us, event | category | flops | bytes accessed | tf_op | source)
XLA Modules:
  0.0 93.7 jit_solution(5449454619522051040)
XLA Ops:
  0.0 0.0 copy-start
  0.7 1.6 %shard_map.82 = (bf16[64,4224]{1,0:T(8,128)(2,1)S(1)}, bf16[32,4224]{1,0:T(8,128)(2,1)S(1)}, bf16[32,4224]{1,0:T(8,128)(2,1)S(1)}) custom-call(s32[1]{0:T(128)S(6)} %copy.9.slot_ref, bf16[1,2,64,4096]{3,2,1,0:T(8,128)(2,1)} %stash_ref.1, s32[1,2,64]{2,1,0:T(2,128)} %doc_ref.1, bf16[32,128]{1,0:T(8,128)(2,1)} %bitcast.1), custom_call_target="tpu_custom_call" | custom-call | tf_op jit(solution)/shard_map/pallas_call | solution.py:74
  2.3 2.6 %collective-permute-start.2 = (bf16[64,4224]{1,0:T(8,128)(2,1)S(1)}, bf16[64,4224]{1,0:T(8,128)(2,1)S(1)}, u32[]{:S(2)}, u32[]{:S(2)}) collective-permute-start(bf16[64,4224]{1,0:T(8,128)(2,1)S(1)} %get-tuple-element.13), channel_id=1, source_target_pairs={{0,1},{1,0},{2,3},{3,2},{4,5},{5,4},{6,7},{7,6},{8,9},{9,8},{10,11... | collective-permute-start | bytes 1622024 | tf_op jit(solution)/shard_map/ppermute | solution.py:303
  4.9 1.5 %collective-permute-done.2 = bf16[64,4224]{1,0:T(8,128)(2,1)S(1)} collective-permute-done((bf16[64,4224]{1,0:T(8,128)(2,1)S(1)}, bf16[64,4224]{1,0:T(8,128)(2,1)S(1)}, u32[]{:S(2)}, u32[]{:S(2)}) %collective-permute-start.2) | collective-permute-done | bytes 540704 | tf_op jit(solution)/shard_map/ppermute | solution.py:303
  6.4 17.0 %collective-permute-start.3 = (bf16[64,4224]{1,0:T(8,128)(2,1)S(1)}, bf16[64,4224]{1,0:T(8,128)(2,1)S(1)}, u32[]{:S(2)}, u32[]{:S(2)}) collective-permute-start(bf16[64,4224]{1,0:T(8,128)(2,1)S(1)} %collective-permute-done.2), channel_id=1, source_target_pairs={{0,8},{1,15},{2,10},{3,9},{4,12},{5,11},{6,14},{7,13},{8,18},{9,17... | collective-permute-start | bytes 1622024 | tf_op jit(solution)/shard_map/ppermute | solution.py:303
  23.5 3.4 %collective-permute-start = (bf16[32,4224]{1,0:T(8,128)(2,1)S(1)}, bf16[32,4224]{1,0:T(8,128)(2,1)S(1)}, u32[]{:S(2)}, u32[]{:S(2)}) collective-permute-start(bf16[32,4224]{1,0:T(8,128)(2,1)S(1)} %get-tuple-element.11), channel_id=1, source_target_pairs={{0,8},{1,15},{2,10},{3,9},{4,12},{5,11},{6,14},{7,13},{8,18},{9,17... | collective-permute-start | bytes 811016 | tf_op jit(solution)/shard_map/ppermute | solution.py:303
  26.9 1.9 %collective-permute-start.1 = (bf16[32,4224]{1,0:T(8,128)(2,1)S(1)}, bf16[32,4224]{1,0:T(8,128)(2,1)S(1)}, u32[]{:S(2)}, u32[]{:S(2)}) collective-permute-start(bf16[32,4224]{1,0:T(8,128)(2,1)S(1)} %get-tuple-element.12), channel_id=1, source_target_pairs={{0,8},{1,15},{2,10},{3,9},{4,12},{5,11},{6,14},{7,13},{8,18},{9,17... | collective-permute-start | bytes 811016 | tf_op jit(solution)/shard_map/ppermute | solution.py:303
  28.8 3.9 %collective-permute-done.refs_0_ = bf16[32,4224]{1,0:T(8,128)(2,1)S(1)} collective-permute-done((bf16[32,4224]{1,0:T(8,128)(2,1)S(1)}, bf16[32,4224]{1,0:T(8,128)(2,1)S(1)}, u32[]{:S(2)}, u32[]{:S(2)}) %collective-permute-start) | collective-permute-done | bytes 270368 | tf_op jit(solution)/shard_map/ppermute | solution.py:303
  32.7 5.0 %collective-permute-done.1.refs_1_ = bf16[32,4224]{1,0:T(8,128)(2,1)S(1)} collective-permute-done((bf16[32,4224]{1,0:T(8,128)(2,1)S(1)}, bf16[32,4224]{1,0:T(8,128)(2,1)S(1)}, u32[]{:S(2)}, u32[]{:S(2)}) %collective-permute-start.1) | collective-permute-done | bytes 270368 | tf_op jit(solution)/shard_map/ppermute | solution.py:303
  37.6 0.0 collective-permute-done.3.refs_2_
  37.6 0.1 shard_map.83.b0
  37.7 13.4 %collective-permute-start.4 = (bf16[128,4224]{1,0:T(8,128)(2,1)S(1)}, bf16[128,4224]{1,0:T(8,128)(2,1)S(1)}, u32[]{:S(2)}, u32[]{:S(2)}) collective-permute-start(bf16[128,4224]{1,0:T(8,128)(2,1)S(1)} %shard_map.83.b0), channel_id=1, source_target_pairs={{0,1},{1,0},{2,3},{3,2},{4,5},{5,4},{6,7},{7,6},{8,9},{9,8},{10,11... | collective-permute-start | bytes 3244040 | tf_op jit(solution)/shard_map/ppermute | solution.py:303
  51.1 1.9 %collective-permute-start.8 = (bf16[64,4224]{1,0:T(8,128)(2,1)S(1)}, bf16[64,4224]{1,0:T(8,128)(2,1)S(1)}, u32[]{:S(2)}, u32[]{:S(2)}) collective-permute-start(bf16[64,4224]{1,0:T(8,128)(2,1)S(1)} %collective-permute-done.3.refs_2_), channel_id=1, source_target_pairs={{0,2},{1,7},{2,4},{3,1},{4,6},{5,3},{6,0},{7,5},{8,10},{9,15},{10,... | collective-permute-start | bytes 1622024 | tf_op jit(solution)/shard_map/ppermute | solution.py:303
  53.0 1.9 %collective-permute-start.5 = (bf16[32,4224]{1,0:T(8,128)(2,1)S(1)}, bf16[32,4224]{1,0:T(8,128)(2,1)S(1)}, u32[]{:S(2)}, u32[]{:S(2)}) collective-permute-start(bf16[32,4224]{1,0:T(8,128)(2,1)S(1)} %collective-permute-done.refs_0_), channel_id=1, source_target_pairs={{0,2},{1,7},{2,4},{3,1},{4,6},{5,3},{6,0},{7,5},{8,10},{9,15},{10,... | collective-permute-start | bytes 811016 | tf_op jit(solution)/shard_map/ppermute | solution.py:303
  55.0 1.9 %collective-permute-start.6 = (bf16[32,4224]{1,0:T(8,128)(2,1)S(1)}, bf16[32,4224]{1,0:T(8,128)(2,1)S(1)}, u32[]{:S(2)}, u32[]{:S(2)}) collective-permute-start(bf16[32,4224]{1,0:T(8,128)(2,1)S(1)} %collective-permute-done.1.refs_1_), channel_id=1, source_target_pairs={{0,2},{1,7},{2,4},{3,1},{4,6},{5,3},{6,0},{7,5},{8,10},{9,15},{10,... | collective-permute-start | bytes 811016 | tf_op jit(solution)/shard_map/ppermute | solution.py:303
  56.9 14.3 %collective-permute-done.5.refs_0_ = bf16[32,4224]{1,0:T(8,128)(2,1)S(1)} collective-permute-done((bf16[32,4224]{1,0:T(8,128)(2,1)S(1)}, bf16[32,4224]{1,0:T(8,128)(2,1)S(1)}, u32[]{:S(2)}, u32[]{:S(2)}) %collective-permute-start.5) | collective-permute-done | bytes 270368 | tf_op jit(solution)/shard_map/ppermute | solution.py:303
  71.2 2.9 %collective-permute-done.6.refs_1_ = bf16[32,4224]{1,0:T(8,128)(2,1)S(1)} collective-permute-done((bf16[32,4224]{1,0:T(8,128)(2,1)S(1)}, bf16[32,4224]{1,0:T(8,128)(2,1)S(1)}, u32[]{:S(2)}, u32[]{:S(2)}) %collective-permute-start.6) | collective-permute-done | bytes 270368 | tf_op jit(solution)/shard_map/ppermute | solution.py:303
  74.2 8.3 %collective-permute-start.7 = (bf16[64,4224]{1,0:T(8,128)(2,1)S(1)}, bf16[64,4224]{1,0:T(8,128)(2,1)S(1)}, u32[]{:S(2)}, u32[]{:S(2)}) collective-permute-start(bf16[64,4224]{1,0:T(8,128)(2,1)S(1)} %shard_map.86.b0), channel_id=1, source_target_pairs={{0,1},{1,0},{2,3},{3,2},{4,5},{5,4},{6,7},{7,6},{8,9},{9,8},{10,11... | collective-permute-start | bytes 1622024 | tf_op jit(solution)/shard_map/ppermute | solution.py:303
  82.5 0.0 collective-permute-done.8.b0
  82.5 1.9 %collective-permute-start.9 = (bf16[64,4224]{1,0:T(8,128)(2,1)S(1)}, bf16[64,4224]{1,0:T(8,128)(2,1)S(1)}, u32[]{:S(2)}, u32[]{:S(2)}) collective-permute-start(bf16[64,4224]{1,0:T(8,128)(2,1)S(1)} %collective-permute-done.8.b0), channel_id=1, source_target_pairs={{0,1},{1,0},{2,3},{3,2},{4,5},{5,4},{6,7},{7,6},{8,9},{9,8},{10,11... | collective-permute-start | bytes 1622024 | tf_op jit(solution)/shard_map/ppermute | solution.py:303
  84.4 0.0 copy-done
  84.4 2.8 %shard_map.84 = (f32[512,128]{1,0:T(8,128)S(1)}, f32[512,128]{1,0:T(8,128)S(1)}, bf16[4096,768]{1,0:T(8,128)(2,1)S(1)}) custom-call(f32[1,128]{1,0:T(1,128)S(1)} %copy-done, bf16[4096,512]{1,0:T(8,128)(2,1)} %w_query.1, bf16[4096,128]{1,0:T(8,128)(2,1)} %w_key.1, bf16[4096,128]{1,0:T(8,128)(2,1)} %w_value.1), custom_call_target="tpu_custom_call" | custom-call | flops 4194304 | bytes 8388608 | tf_op jit(solution)/shard_map/pallas_call | solution.py:119
  87.3 0.0 collective-permute-done.7.b1
  87.3 1.1 %shard_map.87.e1 = bf16[128,896]{1,0:T(8,128)(2,1)S(1)} custom-call(bf16[64,4224]{1,0:T(8,128)(2,1)S(1)} %shard_map.86.b0, bf16[64,4224]{1,0:T(8,128)(2,1)S(1)} %collective-permute-done.7.b1, bf16[4096,768]{1,0:T(8,128)(2,1)S(1)} %get-tuple-element.14.weights, f32[512,128]{1,0:T(8,128)S(1)} %get-tuple-element.15.cosine, f32[512,128]{1,0:T(8,128)S(1)} %get-tuple-element.16.sine), custom_call_target="tpu_custom_call" | custom-call | flops 805306368 | bytes 8388608 | tf_op jit(solution)/shard_map/pallas_call | solution.py:179
  88.3 0.0 collective-permute-done.4.b1
  88.4 1.9 %shard_map.85.e0 = bf16[256,896]{1,0:T(8,128)(2,1)S(1)} custom-call(bf16[128,4224]{1,0:T(8,128)(2,1)S(1)} %shard_map.83.b0, bf16[128,4224]{1,0:T(8,128)(2,1)S(1)} %collective-permute-done.4.b1, bf16[4096,768]{1,0:T(8,128)(2,1)S(1)} %get-tuple-element.14.weights, f32[512,128]{1,0:T(8,128)S(1)} %get-tuple-element.15.cosine, f32[512,128]{1,0:T(8,128)S(1)} %get-tuple-element.16.sine), custom_call_target="tpu_custom_call" | custom-call | flops 1610612736 | bytes 8388608 | tf_op jit(solution)/shard_map/pallas_call | solution.py:179
  90.3 0.0 collective-permute-done.9.b1
  90.3 3.4 %shard_map.88 = bf16[1,512,512]{2,1,0:T(8,128)(2,1)} custom-call(bf16[256,896]{1,0:T(8,128)(2,1)S(1)} %shard_map.85.e0, bf16[128,896]{1,0:T(8,128)(2,1)S(1)} %shard_map.87.e1, bf16[64,4224]{1,0:T(8,128)(2,1)S(1)} %collective-permute-done.8.b0, bf16[64,4224]{1,0:T(8,128)(2,1)S(1)} %collective-permute-done.9.b1, ...), custom_call_target="tpu_custom_call" | custom-call | flops 536870912 | bytes 10485760 | tf_op jit(solution)/shard_map/pallas_call | solution.py:251
  (1 shorter events, 0.0 us)
Async XLA Ops:
  0.0 84.4 %copy-start = (f32[1,128]{1,0:T(1,128)S(1)}, f32[1,128]{1,0:T(1,128)}, u32[]{:S(2)}) copy-start(f32[1,128]{1,0:T(1,128)} %constant.2.clone.inverse_ref) | copy-start | bytes 1540
  2.3 4.1 %collective-permute-start.2 = (bf16[64,4224]{1,0:T(8,128)(2,1)S(1)}, bf16[64,4224]{1,0:T(8,128)(2,1)S(1)}, u32[]{:S(2)}, u32[]{:S(2)}) collective-permute-start(bf16[64,4224]{1,0:T(8,128)(2,1)S(1)} %get-tuple-element.13), channel_id=1, source_target_pairs={{0,1},{1,0},{2,3},{3,2},{4,5},{5,4},{6,7},{7,6},{8,9},{9,8},{10,11... | collective-permute-start | bytes 1622024 | tf_op jit(solution)/shard_map/ppermute | solution.py:303
  6.4 31.2 %collective-permute-start.3 = (bf16[64,4224]{1,0:T(8,128)(2,1)S(1)}, bf16[64,4224]{1,0:T(8,128)(2,1)S(1)}, u32[]{:S(2)}, u32[]{:S(2)}) collective-permute-start(bf16[64,4224]{1,0:T(8,128)(2,1)S(1)} %collective-permute-done.2), channel_id=1, source_target_pairs={{0,8},{1,15},{2,10},{3,9},{4,12},{5,11},{6,14},{7,13},{8,18},{9,17... | collective-permute-start | bytes 1622024 | tf_op jit(solution)/shard_map/ppermute | solution.py:303
  23.5 9.2 %collective-permute-start = (bf16[32,4224]{1,0:T(8,128)(2,1)S(1)}, bf16[32,4224]{1,0:T(8,128)(2,1)S(1)}, u32[]{:S(2)}, u32[]{:S(2)}) collective-permute-start(bf16[32,4224]{1,0:T(8,128)(2,1)S(1)} %get-tuple-element.11), channel_id=1, source_target_pairs={{0,8},{1,15},{2,10},{3,9},{4,12},{5,11},{6,14},{7,13},{8,18},{9,17... | collective-permute-start | bytes 811016 | tf_op jit(solution)/shard_map/ppermute | solution.py:303
  26.9 10.8 %collective-permute-start.1 = (bf16[32,4224]{1,0:T(8,128)(2,1)S(1)}, bf16[32,4224]{1,0:T(8,128)(2,1)S(1)}, u32[]{:S(2)}, u32[]{:S(2)}) collective-permute-start(bf16[32,4224]{1,0:T(8,128)(2,1)S(1)} %get-tuple-element.12), channel_id=1, source_target_pairs={{0,8},{1,15},{2,10},{3,9},{4,12},{5,11},{6,14},{7,13},{8,18},{9,17... | collective-permute-start | bytes 811016 | tf_op jit(solution)/shard_map/ppermute | solution.py:303
  37.7 50.6 %collective-permute-start.4 = (bf16[128,4224]{1,0:T(8,128)(2,1)S(1)}, bf16[128,4224]{1,0:T(8,128)(2,1)S(1)}, u32[]{:S(2)}, u32[]{:S(2)}) collective-permute-start(bf16[128,4224]{1,0:T(8,128)(2,1)S(1)} %shard_map.83.b0), channel_id=1, source_target_pairs={{0,1},{1,0},{2,3},{3,2},{4,5},{5,4},{6,7},{7,6},{8,9},{9,8},{10,11... | collective-permute-start | bytes 3244040 | tf_op jit(solution)/shard_map/ppermute | solution.py:303
  51.1 31.4 %collective-permute-start.8 = (bf16[64,4224]{1,0:T(8,128)(2,1)S(1)}, bf16[64,4224]{1,0:T(8,128)(2,1)S(1)}, u32[]{:S(2)}, u32[]{:S(2)}) collective-permute-start(bf16[64,4224]{1,0:T(8,128)(2,1)S(1)} %collective-permute-done.3.refs_2_), channel_id=1, source_target_pairs={{0,2},{1,7},{2,4},{3,1},{4,6},{5,3},{6,0},{7,5},{8,10},{9,15},{10,... | collective-permute-start | bytes 1622024 | tf_op jit(solution)/shard_map/ppermute | solution.py:303
  53.0 18.2 %collective-permute-start.5 = (bf16[32,4224]{1,0:T(8,128)(2,1)S(1)}, bf16[32,4224]{1,0:T(8,128)(2,1)S(1)}, u32[]{:S(2)}, u32[]{:S(2)}) collective-permute-start(bf16[32,4224]{1,0:T(8,128)(2,1)S(1)} %collective-permute-done.refs_0_), channel_id=1, source_target_pairs={{0,2},{1,7},{2,4},{3,1},{4,6},{5,3},{6,0},{7,5},{8,10},{9,15},{10,... | collective-permute-start | bytes 811016 | tf_op jit(solution)/shard_map/ppermute | solution.py:303
  55.0 19.2 %collective-permute-start.6 = (bf16[32,4224]{1,0:T(8,128)(2,1)S(1)}, bf16[32,4224]{1,0:T(8,128)(2,1)S(1)}, u32[]{:S(2)}, u32[]{:S(2)}) collective-permute-start(bf16[32,4224]{1,0:T(8,128)(2,1)S(1)} %collective-permute-done.1.refs_1_), channel_id=1, source_target_pairs={{0,2},{1,7},{2,4},{3,1},{4,6},{5,3},{6,0},{7,5},{8,10},{9,15},{10,... | collective-permute-start | bytes 811016 | tf_op jit(solution)/shard_map/ppermute | solution.py:303
  74.2 13.1 %collective-permute-start.7 = (bf16[64,4224]{1,0:T(8,128)(2,1)S(1)}, bf16[64,4224]{1,0:T(8,128)(2,1)S(1)}, u32[]{:S(2)}, u32[]{:S(2)}) collective-permute-start(bf16[64,4224]{1,0:T(8,128)(2,1)S(1)} %shard_map.86.b0), channel_id=1, source_target_pairs={{0,1},{1,0},{2,3},{3,2},{4,5},{5,4},{6,7},{7,6},{8,9},{9,8},{10,11... | collective-permute-start | bytes 1622024 | tf_op jit(solution)/shard_map/ppermute | solution.py:303
  82.5 7.8 %collective-permute-start.9 = (bf16[64,4224]{1,0:T(8,128)(2,1)S(1)}, bf16[64,4224]{1,0:T(8,128)(2,1)S(1)}, u32[]{:S(2)}, u32[]{:S(2)}) collective-permute-start(bf16[64,4224]{1,0:T(8,128)(2,1)S(1)} %collective-permute-done.8.b0), channel_id=1, source_target_pairs={{0,1},{1,0},{2,3},{3,2},{4,5},{5,4},{6,7},{7,6},{8,9},{9,8},{10,11... | collective-permute-start | bytes 1622024 | tf_op jit(solution)/shard_map/ppermute | solution.py:303
